TPU v7x, 128 devices: a whole 4x4x4 slice. The times are simulated.
128 devices in a mesh: dp: 16 (over z, y), ep: 8 (over x, core).
Axes of the slice: x: 4, y: 4, z: 4, core: 2. Of those that a mesh axis runs over, the one named last changes fastest.
Arguments:
- hidden: bfloat16 [8192, 2304], P(('dp', 'ep'))
- grad_out: bfloat16 [8192, 2304], P(('dp', 'ep'))
- expert_ids: int32 [8192, 2], P(('dp', 'ep'))
- norm_gain: float32 [2304], replicated
- w_router: float32 [2304, 8], replicated
- w_gate: bfloat16 [8, 2304, 5760], P('ep')
- w_up: bfloat16 [8, 2304, 5760], P('ep')
- w_down: bfloat16 [8, 5760, 2304], P('ep')
Outputs:
- output 1: bfloat16 [8192, 2304], P(('dp', 'ep'))
- output 2: float32 [], replicated
- output 3: bfloat16 [8192, 2304], P(('dp', 'ep'))
- output 4: float32 [2304], replicated
- output 5: float32 [2304, 8], replicated
- output 6: bfloat16 [8, 2304, 5760], P('ep')
- output 7: bfloat16 [8, 2304, 5760], P('ep')
- output 8: bfloat16 [8, 5760, 2304], P('ep')
All inputs are finite; a program needn't handle non-finite values.
Results may differ from a plain program's by a relative error of at most 0.0141986.
Values are sent between devices in bfloat16 or wider.
A program may use at most 1 GiB of HBM per device.

v0:
```python
import functools
import jax
import jax.numpy as jnp
from jax import lax
from jax.experimental import pallas as pl
from jax.experimental.pallas import tpu as pltpu
from jax.sharding import PartitionSpec as P

EPS = 1e-6
AUX_COEF = 0.001
ROWS = 256
GROUP = 2
CHUNK = 512
STRIP = 512
BUFFERS = 3
OWN_TILE = 640
TILE = 384
SLICE = 192
NT = (((1,), (1,)), ((), ()))


def route_tables(expert_ids, n_exp, capacity):
    flat_ids = expert_ids.reshape(-1)
    n_choice = flat_ids.shape[0]
    one_hot = (flat_ids[:, None] == jnp.arange(n_exp, dtype=jnp.int32)[None, :]).astype(jnp.int32)
    running = jnp.cumsum(one_hot, axis=0) - 1
    dest_rows = flat_ids * capacity + jnp.sum(running * one_hot, axis=1)
    slot_owner = jnp.full((n_exp * capacity,), n_choice, jnp.int32).at[dest_rows].set(jnp.arange(n_choice, dtype=jnp.int32))
    return dest_rows, slot_owner


def pack_kernel(block_of, chunk_of, n_steps, my_exp, tok_hbm, pos_ref, wr_ref, x_ref, d_ref, acc, ring, sems):
    step = pl.program_id(0)
    rows, width = x_ref.shape
    block = block_of[step]
    active = step < n_steps[0]
    chunk = chunk_of[step]
    last_chunk = chunk_of[n_steps[0] - 1]

    def load(c):
        slot = lax.rem(c, BUFFERS)
        return pltpu.make_async_copy(tok_hbm.at[pl.ds(pl.multiple_of(c * CHUNK, CHUNK), CHUNK)], ring.at[slot], sems.at[slot])

    @pl.when(step == 0)
    def _():
        for c in range(BUFFERS - 1):
            pl.when(c <= last_chunk)(load(c).start)

    @pl.when(active & ((step == 0) | (chunk != chunk_of[jnp.maximum(step - 1, 0)])))
    def _():
        load(chunk).wait()
        pl.when(chunk + BUFFERS - 1 <= last_chunk)(load(chunk + BUFFERS - 1).start)

    tok_ref = ring.at[lax.rem(chunk, BUFFERS)]
    new = (step == 0) | (block != block_of[jnp.maximum(step - 1, 0)])

    @pl.when(active)
    def _():
        row_id = block * rows + lax.broadcasted_iota(jnp.int32, (rows, tok_ref.shape[0]), 0)
        hit = (pos_ref[0] == row_id).astype(jnp.float32).astype(jnp.bfloat16)
        for at in range(0, 2 * width, STRIP):
            cols = slice(at, at + STRIP)
            acc[:, cols] = jnp.where(new, 0.0, acc[:, cols]) + jnp.dot(hit, tok_ref[:, cols], preferred_element_type=jnp.float32)

    @pl.when((step == n_steps[0] - 1) | (active & (block != block_of[step + 1])))
    def _():
        x = acc[:, :width].astype(jnp.bfloat16)
        logits = jnp.dot(x, wr_ref[...], preferred_element_type=jnp.float32)
        lane = lax.broadcasted_iota(jnp.int32, logits.shape, 1)
        logits = jnp.where(lane < my_exp[1], logits, -jnp.inf)
        p = jnp.exp(logits - jnp.max(logits, axis=1, keepdims=True))
        gate = jnp.sum(jnp.where(lane == my_exp[0], p, 0.0), axis=1, keepdims=True) / jnp.sum(p, axis=1, keepdims=True)
        x_ref[...] = x
        d_ref[...] = (acc[:, width:] * gate).astype(jnp.bfloat16)


def pack_rows(tokens, width, mask, w_router, my_exp, cap):
    n_tok = tokens.shape[0]
    n_exp = w_router.shape[1]
    n_chunk = n_tok // CHUNK
    n_block = cap // ROWS
    m = mask.astype(jnp.bfloat16).reshape(n_chunk, CHUNK)
    idx = jnp.arange(CHUNK)
    inside = jnp.dot(m, (idx[:, None] < idx[None, :]).astype(jnp.bfloat16), preferred_element_type=jnp.float32).astype(jnp.int32)
    per_chunk = jnp.sum(mask.astype(jnp.int32).reshape(n_chunk, CHUNK), axis=1)
    cidx = jnp.arange(n_chunk)
    ends = jnp.sum(jnp.where(cidx[None, :] <= cidx[:, None], per_chunk[None, :], 0), axis=1)
    pos = jnp.where(mask.reshape(n_chunk, CHUNK), inside + (ends - per_chunk)[:, None], -1)
    count = jnp.sum(per_chunk)
    n_used = jnp.maximum((count + ROWS - 1) // ROWS, 1)
    bidx = jnp.arange(n_block)
    last_row = jnp.minimum((bidx + 1) * ROWS, count) - 1
    last_chunk = jnp.sum((ends[None, :] <= last_row[:, None]).astype(jnp.int32), axis=1)
    n_steps = jnp.sum(jnp.where(bidx == n_used - 1, last_chunk + bidx, 0)) + 1
    steps = jnp.arange(n_chunk + n_block + 1)
    block_of = jnp.minimum(jnp.sum(((last_chunk + bidx)[None, :] < steps[:, None]).astype(jnp.int32), axis=1), n_used - 1)
    chunk_of = jnp.clip(steps - block_of, 0, n_chunk - 1)
    chunk_of = jnp.where(steps < n_steps, chunk_of, n_chunk - 1)
    grid_spec = pltpu.PrefetchScalarGridSpec(
        num_scalar_prefetch=4,
        grid=(n_chunk + n_block,),
        in_specs=[
            pl.BlockSpec(memory_space=pl.ANY),
            pl.BlockSpec((1, 1, CHUNK), lambda s, b, c, n, e: (c[s], 0, 0)),
            pl.BlockSpec((width, 128), lambda s, b, c, n, e: (0, 0)),
        ],
        out_specs=[pl.BlockSpec((ROWS, width), lambda s, b, c, n, e: (b[s], 0))] * 2,
        scratch_shapes=[
            pltpu.VMEM((ROWS, 2 * width), jnp.float32),
            pltpu.VMEM((BUFFERS, CHUNK, 2 * width), jnp.bfloat16),
            pltpu.SemaphoreType.DMA((BUFFERS,)),
        ],
    )
    x_rows, d_rows = pl.pallas_call(
        pack_kernel,
        grid_spec=grid_spec,
        out_shape=[jax.ShapeDtypeStruct((cap, width), jnp.bfloat16)] * 2,
        compiler_params=pltpu.CompilerParams(dimension_semantics=("arbitrary",), vmem_limit_bytes=56 * 2**20),
        cost_estimate=pl.CostEstimate(flops=5 * CHUNK * cap * width, bytes_accessed=n_tok * width * 5, transcendentals=0),
        name="pack_rows",
    )(
        block_of.astype(jnp.int32),
        chunk_of.astype(jnp.int32),
        n_steps.astype(jnp.int32)[None],
        jnp.stack([my_exp, jnp.int32(n_exp)]),
        tokens,
        pos.astype(jnp.int32)[:, None, :],
        jnp.pad(w_router, ((0, 0), (0, 128 - n_exp))).astype(jnp.bfloat16),
    )
    return x_rows, d_rows, n_used.astype(jnp.int32)


def ffn_grads(hg, hu, da):
    hg, hu, da = (v.astype(jnp.bfloat16).astype(jnp.float32) for v in (hg, hu, da))
    sig = jax.nn.sigmoid(hg)
    silu = hg * sig
    act = (silu * hu).astype(jnp.bfloat16)
    dhu = (da * silu).astype(jnp.bfloat16)
    dhg = (da * hu * sig * (1.0 + hg * (1.0 - sig))).astype(jnp.bfloat16)
    return act, dhg, dhu


def own_kernel(r_ref, wg_ref, wu_ref, wd_ref, out_ref, wt_ref, acc_o, acc_x):
    j = pl.program_id(0)
    width = wd_ref.shape[1]
    x, d = r_ref[:, :width], r_ref[:, width:]

    @pl.when(j == 0)
    def _():
        acc_o[...] = jnp.zeros_like(acc_o)
        acc_x[...] = jnp.zeros_like(acc_x)

    wt_ref[0] = wg_ref[...].T
    wt_ref[1] = wu_ref[...].T
    hg = jnp.dot(x, wg_ref[...], preferred_element_type=jnp.float32)
    hu = jnp.dot(x, wu_ref[...], preferred_element_type=jnp.float32)
    da = lax.dot_general(wd_ref[...], d, NT, preferred_element_type=jnp.float32).astype(jnp.bfloat16).T
    act, dhg, dhu = ffn_grads(hg, hu, da)
    strip = width // 3 if width % 384 == 0 else width

    def add(i, carry):
        part = pl.ds(pl.multiple_of(i * strip, 128), strip)
        acc_o[:, part] += jnp.dot(act, wd_ref[:, part], preferred_element_type=jnp.float32)
        acc_x[part] += lax.dot_general(wg_ref[part], dhg, NT, preferred_element_type=jnp.float32) + lax.dot_general(wu_ref[part], dhu, NT, preferred_element_type=jnp.float32)
        return carry

    lax.fori_loop(0, width // strip, add, 0)

    @pl.when(j == pl.num_programs(0) - 1)
    def _():
        out_ref[:, :width] = acc_o[...].astype(jnp.bfloat16)
        out_ref[:, width:] = acc_x[...].astype(jnp.bfloat16).T


def own_rows(recv, w_gate, w_up, w_down):
    rows, two_d = recv.shape
    width, ff = w_gate.shape
    f = OWN_TILE
    whole = pl.BlockSpec((rows, two_d), lambda j: (0, 0))
    col_spec = pl.BlockSpec((width, f), lambda j: (0, j))
    return pl.pallas_call(
        own_kernel,
        grid=(ff // f,),
        in_specs=[whole, col_spec, col_spec, pl.BlockSpec((f, width), lambda j: (j, 0))],
        out_specs=[whole, pl.BlockSpec((2, f, width), lambda j: (0, j, 0))],
        out_shape=[jax.ShapeDtypeStruct((rows, two_d), jnp.bfloat16), jax.ShapeDtypeStruct((2, ff, width), jnp.bfloat16)],
        scratch_shapes=[pltpu.VMEM((rows, width), jnp.float32), pltpu.VMEM((width, rows), jnp.float32)],
        compiler_params=pltpu.CompilerParams(dimension_semantics=("arbitrary",), vmem_limit_bytes=62 * 2**20),
        cost_estimate=pl.CostEstimate(flops=12 * rows * width * ff, bytes_accessed=6 * width * ff, transcendentals=0),
        name="own_rows",
    )(recv, w_gate, w_up, w_down)


def tile_kernel(transpose, n_used, tile_of, block_of, x_ref, d_ref, wt_ref, wd_ref, *rest):
    outs, (acc_gu, acc_d, dgus, acts) = rest[:-4], rest[-4:]
    f = wd_ref.shape[0]
    step = pl.program_id(0)
    block = block_of[step]
    active = step < n_used[1]
    left = n_used[0] - GROUP * block

    def products(i, carry):
        at = pl.ds(pl.multiple_of(i * ROWS, ROWS), ROWS)
        wt = wt_ref[...].reshape(2 * f, wd_ref.shape[1])
        h = lax.dot_general(wt, x_ref[at], NT, preferred_element_type=jnp.float32)
        da = lax.dot_general(wd_ref[...], d_ref[at], NT, preferred_element_type=jnp.float32)
        acts[:, at], dgus[:f, at], dgus[f:, at] = ffn_grads(h[:f], h[f:], da)
        return carry

    @pl.when(active)
    def _():
        lax.fori_loop(0, jnp.minimum(left, GROUP), products, 0)

    def sums(rows):
        width = wd_ref.shape[1]
        strip = width // 3 if transpose and width % 384 == 0 else width

        def add(i, carry):
            cols = pl.ds(pl.multiple_of(i * strip, 128), strip)
            acc_gu[:, cols] = jnp.where(block == 0, 0.0, acc_gu[:, cols]) + jnp.dot(dgus[:, :rows], x_ref[:rows, cols], preferred_element_type=jnp.float32)
            acc_d[:, cols] = jnp.where(block == 0, 0.0, acc_d[:, cols]) + jnp.dot(acts[:, :rows], d_ref[:rows, cols], preferred_element_type=jnp.float32)
            return carry

        lax.fori_loop(0, width // strip, add, 0)

    for parts in range(1, GROUP + 1):
        fits = left >= parts if parts == GROUP else left == parts
        pl.when(active & fits)(functools.partial(sums, parts * ROWS))

    @pl.when(active & (left <= GROUP))
    def _():
        if transpose:
            outs[0][...] = acc_gu[:f].astype(jnp.bfloat16).T
            outs[1][...] = acc_gu[f:].astype(jnp.bfloat16).T
            outs[2][...] = acc_d[...].astype(jnp.bfloat16)
        else:
            outs[0][:2 * f] = acc_gu[...].astype(jnp.bfloat16)
            outs[0][2 * f:] = acc_d[...].astype(jnp.bfloat16)


def tile_grads(x_rows, d_rows, n_used, wt, wd, f, n_tile, ff):
    cap, width = x_rows.shape
    n_block = cap // (GROUP * ROWS)
    n_group = (n_used + GROUP - 1) // GROUP
    steps = jnp.arange(n_tile * n_block, dtype=jnp.int32)
    tile_of = jnp.minimum(steps // n_group, n_tile - 1)
    block_of = jnp.where(steps < n_tile * n_group, steps % n_group, n_group - 1)
    used = jnp.stack([n_used, n_tile * n_group])
    row_spec = pl.BlockSpec((GROUP * ROWS, width), lambda s, n, t, b: (b[s], 0))
    col_spec = pl.BlockSpec((width, f), lambda s, n, t, b: (0, t[s]))
    down_spec = pl.BlockSpec((f, width), lambda s, n, t, b: (t[s], 0))
    if ff:
        out_specs = [col_spec, col_spec, down_spec]
        out_shape = [jax.ShapeDtypeStruct((width, ff), jnp.bfloat16)] * 2 + [jax.ShapeDtypeStruct((ff, width), jnp.bfloat16)]
    else:
        out_specs = [pl.BlockSpec((3 * f, width), lambda s, n, t, b: (0, 0))]
        out_shape = [jax.ShapeDtypeStruct((3 * f, width), jnp.bfloat16)]
    return pl.pallas_call(
        functools.partial(tile_kernel, bool(ff)),
        grid_spec=pltpu.PrefetchScalarGridSpec(
            num_scalar_prefetch=3,
            grid=(n_tile * n_block,),
            in_specs=[row_spec, row_spec, pl.BlockSpec((2, f, width), lambda s, n, t, b: (0, t[s], 0)), down_spec],
            out_specs=out_specs,
            scratch_shapes=[
                pltpu.VMEM((2 * f, width), jnp.float32),
                pltpu.VMEM((f, width), jnp.float32),
                pltpu.VMEM((2 * f, GROUP * ROWS), jnp.bfloat16),
                pltpu.VMEM((f, GROUP * ROWS), jnp.bfloat16),
            ],
        ),
        out_shape=out_shape,
        compiler_params=pltpu.CompilerParams(dimension_semantics=("arbitrary",), vmem_limit_bytes=63 * 2**20),
        cost_estimate=pl.CostEstimate(flops=12 * (cap // 2) * width * f * n_tile, bytes_accessed=n_tile * cap * width * 2, transcendentals=0),
        name="tile_grads" if ff else "slice_grads",
    )(used, tile_of, block_of, x_rows, d_rows, wt, wd)


def place_kernel(part_ref, gg_in, gu_in, gd_in, gg_ref, gu_ref, gd_ref):
    f = SLICE
    gg_ref[...] = jnp.concatenate([part_ref[0, :f], part_ref[1, :f]], axis=0).T
    gu_ref[...] = jnp.concatenate([part_ref[0, f:2 * f], part_ref[1, f:2 * f]], axis=0).T
    gd_ref[:f] = part_ref[0, 2 * f:]
    gd_ref[f:] = part_ref[1, 2 * f:]


def place_slices(parts, g_gate, g_up, g_down, n_tile):
    n_part, _, width = parts.shape
    col_spec = pl.BlockSpec((width, 2 * SLICE), lambda i: (0, n_tile + i))
    down_spec = pl.BlockSpec((2 * SLICE, width), lambda i: (n_tile + i, 0))
    any_spec = pl.BlockSpec(memory_space=pl.ANY)
    return pl.pallas_call(
        place_kernel,
        grid=(n_part // 2,),
        in_specs=[pl.BlockSpec((2, 3 * SLICE, width), lambda i: (i, 0, 0)), any_spec, any_spec, any_spec],
        out_specs=[col_spec, col_spec, down_spec],
        out_shape=[jax.ShapeDtypeStruct(g.shape, g.dtype) for g in (g_gate, g_up, g_down)],
        input_output_aliases={1: 0, 2: 1, 3: 2},
        compiler_params=pltpu.CompilerParams(dimension_semantics=("arbitrary",), vmem_limit_bytes=50 * 2**20),
        cost_estimate=pl.CostEstimate(flops=10**6, bytes_accessed=4 * parts.size, transcendentals=0),
        name="place_slices",
    )(parts, g_gate, g_up, g_down)


def solution(mesh):
    n_dp, n_ep = mesh.shape["dp"], mesh.shape["ep"]
    n_dev = n_dp * n_ep
    all_axes = ("dp", "ep")

    def local_step(hidden, grad_out, expert_ids, norm_gain, w_router, w_gate, w_up, w_down):
        n_tok, width = hidden.shape
        n_exp = w_router.shape[1]
        capacity = 4 * n_tok // n_exp
        total_tok = n_tok * n_dev
        w_gate, w_up, w_down = w_gate[0], w_up[0], w_down[0]
        ff = w_gate.shape[1]
        n_tile = (ff - SLICE * n_dp) // TILE
        my_exp = lax.axis_index("ep")
        dest_rows, slot_owner = route_tables(expert_ids, n_exp, capacity)
        choice_hot = (expert_ids[:, :, None] == jnp.arange(n_exp, dtype=jnp.int32)).astype(jnp.float32)

        x_f32 = hidden.astype(jnp.float32)
        inv_rms = lax.rsqrt(jnp.mean(x_f32 * x_f32, axis=-1, keepdims=True) + EPS)
        x_hat = x_f32 * inv_rms
        x_norm = (x_hat * norm_gain).astype(jnp.bfloat16)
        xn_f32 = x_norm.astype(jnp.float32)

        tokens = lax.all_gather(jnp.concatenate([x_norm, grad_out], axis=1), all_axes, axis=0, tiled=True)

        router_probs = jax.nn.softmax(jnp.dot(xn_f32, w_router, preferred_element_type=jnp.float32), axis=-1)
        gate_vals = jnp.sum(router_probs[:, None, :] * choice_hot, axis=-1)

        dy_f32 = grad_out.astype(jnp.float32)
        d_picked = (dy_f32[:, None, :] * gate_vals[:, :, None]).astype(jnp.bfloat16).reshape(n_tok * 2, width)
        send_x = jnp.take(x_norm, slot_owner // 2, axis=0, mode="fill", fill_value=0)
        send_d = jnp.take(d_picked, slot_owner, axis=0, mode="fill", fill_value=0)
        send = jnp.concatenate([send_x, send_d], axis=1).reshape(n_exp, capacity, 2 * width)
        recv = lax.all_to_all(send, "ep", 0, 0, tiled=True).reshape(n_exp * capacity, 2 * width)
        home, wt = own_rows(recv, w_gate, w_up, w_down)

        pad = jnp.zeros((n_tok, 16 - n_exp - 2), jnp.float32)
        routes = jnp.concatenate([router_probs, expert_ids.astype(jnp.float32), pad], axis=1)
        routes, home = lax.optimization_barrier((routes, home))
        routes = lax.all_gather(routes, all_axes, axis=0, tiled=True)
        all_probs, all_ids = routes[:, :n_exp], routes[:, n_exp:n_exp + 2].astype(jnp.int32)
        exp_range = jnp.arange(n_exp, dtype=jnp.int32)
        loads = jnp.sum((all_ids[:, 0:1] == exp_range).astype(jnp.float32) + (all_ids[:, 1:2] == exp_range).astype(jnp.float32), axis=0)
        load_frac = loads / (2 * total_tok)
        aux_loss = AUX_COEF * n_exp * jnp.sum(load_frac * jnp.sum(all_probs, axis=0) / total_tok)

        home = home.reshape(n_exp, capacity, 2 * width)
        back = lax.all_to_all(home, "ep", 0, 0, tiled=True).reshape(n_exp * capacity, 2 * width)
        taken = jnp.take(back, dest_rows, axis=0).reshape(n_tok, 2, 2 * width)
        picked, d_xn_exp = taken[:, :, :width], taken[:, :, width:]
        out_hidden = (x_f32 + jnp.sum(gate_vals[:, :, None] * picked, axis=1)).astype(jnp.bfloat16)

        d_gates = jnp.sum(dy_f32[:, None, :] * picked, axis=-1)
        d_probs = jnp.sum(d_gates[:, :, None] * choice_hot, axis=1) + (AUX_COEF * n_exp / total_tok) * load_frac
        d_logits = router_probs * (d_probs - jnp.sum(router_probs * d_probs, axis=-1, keepdims=True))
        d_xnorm = jnp.einsum("te,de->td", d_logits, w_router) + d_xn_exp[:, 0].astype(jnp.float32) + d_xn_exp[:, 1].astype(jnp.float32)
        d_xnorm = d_xnorm.astype(jnp.bfloat16).astype(jnp.float32)
        scaled = d_xnorm * norm_gain
        grad_hidden = (inv_rms * (scaled - x_hat * jnp.mean(scaled * x_hat, axis=-1, keepdims=True)) + dy_f32).astype(jnp.bfloat16)
        small = [jnp.sum(d_xnorm * x_hat, axis=0), jnp.einsum("te,td->ed", d_logits, xn_f32).reshape(-1)]
        small = lax.all_gather(jnp.concatenate(small).reshape(-1, 128), all_axes, axis=0, tiled=True)
        small = jnp.sum(small.reshape(n_dev, -1, 128), axis=0).reshape(1 + n_exp, width)

        at = n_tile * TILE + SLICE * lax.axis_index("dp")
        wt_mine = lax.dynamic_slice(wt, (0, at, 0), (2, SLICE, width))
        wd_mine = lax.dynamic_slice(w_down, (at, 0), (SLICE, width))
        names = all_ids == my_exp
        x_rows, do_rows, n_used = pack_rows(tokens, width, names[:, 0] | names[:, 1], w_router, my_exp, n_dev * capacity)
        (mine,) = tile_grads(x_rows, do_rows, n_used, wt_mine, wd_mine, SLICE, 1, 0)
        parts = lax.all_gather(mine, "dp", axis=0, tiled=False)
        grads = tile_grads(x_rows, do_rows, n_used, wt, w_down, TILE, n_tile, ff)
        g_gate, g_up, g_down = place_slices(parts, *grads, n_tile)
        return (out_hidden, aux_loss, grad_hidden, small[0], small[1:].T, g_gate[None], g_up[None], g_down[None])

    tok_spec = P(all_axes, None)
    w_spec = P("ep", None, None)
    return jax.shard_map(local_step, mesh=mesh, in_specs=(tok_spec, tok_spec, tok_spec, P(), P(), w_spec, w_spec, w_spec), out_specs=(tok_spec, P(), tok_spec, P(), P(), w_spec, w_spec, w_spec), check_vma=False)
```

profile of v0, /device:TPU:1, one launch (start us, length us, event | category | flops | bytes accessed | tf_op | source)
XLA Modules:
  0.0 604.6 jit_solution(11452538269975889620)
XLA Ops:
  7.2 1.1 fusion.18
  8.4 1.1 fusion.11
  9.5 1.9 pad_maximum_fusion.1
  12.3 1.0 scatter_custom_fusion
  14.8 2.4 gather_fusion
  18.5 2.4 gather_fusion.1
  21.1 1.1 copy-done.1
  22.4 1.6 pad_maximum_fusion
  24.0 5.8 all-to-all-start
  31.0 36.7 %all-to-all-done = bf16[8,32,4608]{2,1,0:T(8,128)(2,1)} async-done(((bf16[8,32,4608]{2,1,0:T(8,128)(2,1)}), bf16[8,32,4608]{2,1,0:T(8,128)(2,1)}, u32[]{:S(2)}, u32[]{:S(2)}) %all-to-all-start) | async-done | bytes 2359328 | tf_op jit(solution)/shard_map/all_to_all | solution.py:338
  67.7 66.9 %own_rows.1 = (bf16[256,4608]{1,0:T(8,128)(2,1)}, bf16[2,5760,2304]{2,1,0:T(8,128)(2,1)}) custom-call(bf16[256,4608]{1,0:T(8,128)(2,1)} %bitcast.4.r_ref, bf16[2304,5760]{1,0:T(8,128)(2,1)} %bitcast.64, bf16[2304,5760]{1,0:T(8,128)(2,1)} %bitcast.65, bf16[5760,2304]{1,0:T(8,128)(2,1)} %bitcast.62), custom_call_target="tpu_custom_call" | custom-call | flops 40768634880 | bytes 79626240 | tf_op jit(solution)/shard_map/own_rows/pallas_call | solution.py:181
  134.6 6.3 %all-to-all-start.1 = ((bf16[8,32,4608]{2,1,0:T(8,128)(2,1)}), bf16[8,32,4608]{2,1,0:T(8,128)(2,1)}, u32[]{:S(2)}, u32[]{:S(2)}) async-start(bf16[8,32,4608]{2,1,0:T(8,128)(2,1)} %bitcast.57), calls=%async_computation.1 | async-start | bytes 4718592 | tf_op jit(solution)/shard_map/all_to_all | solution.py:352
  140.9 84.3 %all-gather.1 = f32[128,64,16]{1,2,0:T(8,128)S(1)} all-gather(f32[1,64,16]{1,2,0:T(8,128)S(1)} %bitcast.61), channel_id=1, replica_groups=mesh['dp'=16,'ep'=8] {'dp','ep'}, dimensions={0}, use_global_device_ids=true | all-gather | bytes 528384 | tf_op jit(solution)/shard_map/all_gather | solution.py:344
  226.8 4.4 gather_fusion.2
  233.8 2.0 fusion.17
  238.4 2.1 dynamic-slice_bitcast_fusion.wd_ref
  240.6 1.0 broadcast_compare_fusion
  248.3 2.8 constant_dynamic-slice_fusion.wt_ref
  251.1 48.3 %pack_rows.1 = (bf16[4096,2304]{1,0:T(8,128)(2,1)}, bf16[4096,2304]{1,0:T(8,128)(2,1)}) custom-call(s32[33]{0:T(128)} %get-tuple-element.37.block_of, s32[33]{0:T(128)} %get-tuple-element.36.chunk_of, s32[1]{0:T(128)} %bitcast.20.n_steps, s32[2]{0:T(128)} %pad_add_fusion.1.my_exp, bf16[8192,4608]{1,0:T(8,128)(2,1)} %all-gather.7.cloned.1.call-done.tok_hbm, ...), custom_call_target="tpu_custom_call" | custom-call | flops 24159191040 | bytes 94371840 | tf_op jit(solution)/shard_map/pack_rows/pallas_call | solution.py:114
  299.4 22.8 %slice_grads.1 = bf16[576,2304]{1,0:T(8,128)(2,1)} custom-call(s32[2]{0:T(128)} %pad_add_fusion.n_used, s32[8]{0:T(128)} %get-tuple-element.59.tile_of, s32[8]{0:T(128)} %get-tuple-element.58.block_of, bf16[4096,2304]{1,0:T(8,128)(2,1)} %get-tuple-element.23.x_ref, bf16[4096,2304]{1,0:T(8,128)(2,1)} %get-tuple-element.24.d_ref, ...), custom_call_target="tpu_custom_call" | custom-call | flops 10871635968 | bytes 18874368 | tf_op jit(solution)/shard_map/slice_grads/pallas_call | solution.py:258
  324.4 1.0 fusion.16
  325.4 4.7 reduce_sum.199
  331.3 238.2 %tile_grads.1 = (bf16[2304,5760]{1,0:T(8,128)(2,1)}, bf16[2304,5760]{1,0:T(8,128)(2,1)}, bf16[5760,2304]{1,0:T(8,128)(2,1)}) custom-call(s32[2]{0:T(128)} %pad_add_fusion.2.n_used, s32[56]{0:T(128)} %get-tuple-element.57.tile_of, s32[56]{0:T(128)} %get-tuple-element.56.block_of, bf16[4096,2304]{1,0:T(8,128)(2,1)} %get-tuple-element.23.x_ref, ...), custom_call_target="tpu_custom_call" | custom-call | flops 152202903552 | bytes 132120576 | tf_op jit(solution)/shard_map/tile_grads/pallas_call | solution.py:258
  569.5 27.4 %place_slices.1 = (bf16[2304,5760]{1,0:T(8,128)(2,1)}, bf16[2304,5760]{1,0:T(8,128)(2,1)}, bf16[5760,2304]{1,0:T(8,128)(2,1)}) custom-call(bf16[16,576,2304]{2,1,0:T(8,128)(2,1)} %bitcast.51, bf16[2304,5760]{1,0:T(8,128)(2,1)} %get-tuple-element.26.gg_in, ...), custom_call_target="tpu_custom_call", output_to_operand_aliasing={{0}: (1, {}), {1}: (2, {}), {2}: (3, {})} | custom-call | flops 1000000 | bytes 84934656 | tf_op jit(solution)/shard_map/place_slices/pallas_call | solution.py:292
  (126 shorter events, 19.8 us)
Async XLA Ops:
  7.2 243.9 %all-gather.7.cloned.1.call-start = ((), (), s32[]{:S(2)}) async-start(), calls=%async_computation.2 | async-start | bytes 76087296 | tf_op jit(solution)/shard_map/all_gather | solution.py:328
  8.3 3.0 copy-start.18
  8.4 3.0 copy-start.10
  9.5 4.0 copy-start.8
  14.3 2.9 copy-start.11
  14.8 2.4 copy-start.2
  18.5 2.5 copy-start
  20.9 1.3 copy-start.1
  24.0 43.7 %all-to-all-start = ((bf16[8,32,4608]{2,1,0:T(8,128)(2,1)}), bf16[8,32,4608]{2,1,0:T(8,128)(2,1)}, u32[]{:S(2)}, u32[]{:S(2)}) async-start(bf16[8,32,4608]{2,1,0:T(8,128)(2,1)} %pad_maximum_fusion), calls=%async_computation | async-start | bytes 4718592 | tf_op jit(solution)/shard_map/all_to_all | solution.py:338
  134.6 92.2 %all-to-all-start.1 = ((bf16[8,32,4608]{2,1,0:T(8,128)(2,1)}), bf16[8,32,4608]{2,1,0:T(8,128)(2,1)}, u32[]{:S(2)}, u32[]{:S(2)}) async-start(bf16[8,32,4608]{2,1,0:T(8,128)(2,1)} %bitcast.57), calls=%async_computation.1 | async-start | bytes 4718592 | tf_op jit(solution)/shard_map/all_to_all | solution.py:352
  140.9 184.6 %all-gather.11.cloned.1.call-start = ((), (), s32[]{:S(2)}) async-start(), calls=%async_computation.4 | async-start | bytes 11096064 | tf_op jit(solution)/shard_map/all_gather | solution.py:365
  225.8 0.9 copy-start.6
  226.8 6.7 %copy-start.15 = (f32[8]{0:T(128)}, f32[8]{0:T(128)S(1)}, u32[]{:S(2)}) copy-start(f32[8]{0:T(128)S(1)} %get-tuple-element.51) | copy-start | bytes 100
  231.7 1.1 copy-start.5
  231.7 1.1 copy-start.12
  232.7 0.7 copy-start.14
  232.7 0.7 copy-start.17
  232.7 1.0 copy-start.3
  232.8 1.0 copy-start.9
  232.8 1.0 copy-start.19
  236.5 333.0 %all-gather.9.cloned.1.call-start = ((), (), s32[]{:S(2)}) async-start(), calls=%async_computation.3 | async-start | bytes 45121536 | tf_op jit(solution)/shard_map/all_gather | solution.py:374
  322.2 2.1 copy-start.4
  322.2 2.1 copy-start.7
  322.2 2.1 copy-start.20
  (2 other events, 1.1 us)
Sparse Core Ops, SparseCore 0:
  11.5 218.9 all-gather.6
  236.6 68.5 all-gather.10
  322.4 238.8 all-gather.8
where the time goes:
time: 605 us
  Pallas kernels  404 us (67%)
  blocking collectives  84.3 us (14%)
  waiting for transfers between devices  36.7 us (6%)
  local copies, waits for them, and re-layouts  25 us (4%)
  other arithmetic  22.8 us (4%)
  between operations  17.3 us (3%)
  starting transfers between devices  12.1 us (2%)
    pallas_call x2, Pallas kernels, tile_grads(): pl.pallas_call(functools.partial(tile_kernel, bool(ff)), grid_spec=pltpu....  261 us
    all_gather x1, blocking collectives, local_step(): routes = lax.all_gather(routes, all_axes, axis=0, tiled=True)  84.3 us
    pallas_call x1, Pallas kernels, own_rows(): pl.pallas_call(own_kernel, grid=(ff // f,), in_specs=[whole, col_spec, co...  66.9 us
    pallas_call x1, Pallas kernels, pack_rows(): pl.pallas_call(pack_kernel, grid_spec=grid_spec, out_shape=[jax.ShapeDtyp...  48.3 us
    all_to_all x1, waiting for transfers between devices, local_step(): lax.all_to_all(send, 'ep', 0, 0, tiled=True)  36.7 us
    pallas_call x1, Pallas kernels, place_slices(): pl.pallas_call(place_kernel, grid=(n_part // 2,), in_specs=[pl.BlockSpec(...  27.4 us
  transfers between devices with their start and end apart: 5, of which 1 were waited for; matrix products, arithmetic and copies ran while one was open for 7% of the time, Pallas kernels for 62%

commit v1 on v0

--- a/solution.py
+++ b/solution.py
@@ -39,7 +39,7 @@
 
     def load(c):
         slot = lax.rem(c, BUFFERS)
-        return pltpu.make_async_copy(tok_hbm.at[pl.ds(pl.multiple_of(c * CHUNK, CHUNK), CHUNK)], ring.at[slot], sems.at[slot])
+        return pltpu.make_async_copy(tok_hbm.at[pl.ds(pl.multiple_of(c * CHUNK, CHUNK), CHUNK), pl.ds(0, ring.shape[2])], ring.at[slot], sems.at[slot])
 
     @pl.when(step == 0)
     def _():
@@ -325,7 +325,7 @@
         x_norm = (x_hat * norm_gain).astype(jnp.bfloat16)
         xn_f32 = x_norm.astype(jnp.float32)
 
-        tokens = lax.all_gather(jnp.concatenate([x_norm, grad_out], axis=1), all_axes, axis=0, tiled=True)
+        tokens = lax.all_gather(jnp.concatenate([x_norm, grad_out, jnp.pad(expert_ids.astype(jnp.bfloat16), ((0, 0), (0, 126)))], axis=1), all_axes, axis=0, tiled=True)
 
         router_probs = jax.nn.softmax(jnp.dot(xn_f32, w_router, preferred_element_type=jnp.float32), axis=-1)
         gate_vals = jnp.sum(router_probs[:, None, :] * choice_hot, axis=-1)
@@ -338,22 +338,16 @@
         recv = lax.all_to_all(send, "ep", 0, 0, tiled=True).reshape(n_exp * capacity, 2 * width)
         home, wt = own_rows(recv, w_gate, w_up, w_down)
 
-        pad = jnp.zeros((n_tok, 16 - n_exp - 2), jnp.float32)
-        routes = jnp.concatenate([router_probs, expert_ids.astype(jnp.float32), pad], axis=1)
-        routes, home = lax.optimization_barrier((routes, home))
-        routes = lax.all_gather(routes, all_axes, axis=0, tiled=True)
-        all_probs, all_ids = routes[:, :n_exp], routes[:, n_exp:n_exp + 2].astype(jnp.int32)
         exp_range = jnp.arange(n_exp, dtype=jnp.int32)
-        loads = jnp.sum((all_ids[:, 0:1] == exp_range).astype(jnp.float32) + (all_ids[:, 1:2] == exp_range).astype(jnp.float32), axis=0)
-        load_frac = loads / (2 * total_tok)
-        aux_loss = AUX_COEF * n_exp * jnp.sum(load_frac * jnp.sum(all_probs, axis=0) / total_tok)
-
         home = home.reshape(n_exp, capacity, 2 * width)
         back = lax.all_to_all(home, "ep", 0, 0, tiled=True).reshape(n_exp * capacity, 2 * width)
         taken = jnp.take(back, dest_rows, axis=0).reshape(n_tok, 2, 2 * width)
         picked, d_xn_exp = taken[:, :, :width], taken[:, :, width:]
         out_hidden = (x_f32 + jnp.sum(gate_vals[:, :, None] * picked, axis=1)).astype(jnp.bfloat16)
 
+        all_ids = tokens[:, 2 * width:2 * width + 2].astype(jnp.int32)
+        loads = jnp.sum((all_ids[:, 0:1] == exp_range).astype(jnp.float32) + (all_ids[:, 1:2] == exp_range).astype(jnp.float32), axis=0)
+        load_frac = loads / (2 * total_tok)
         d_gates = jnp.sum(dy_f32[:, None, :] * picked, axis=-1)
         d_probs = jnp.sum(d_gates[:, :, None] * choice_hot, axis=1) + (AUX_COEF * n_exp / total_tok) * load_frac
         d_logits = router_probs * (d_probs - jnp.sum(router_probs * d_probs, axis=-1, keepdims=True))
@@ -361,9 +355,11 @@
         d_xnorm = d_xnorm.astype(jnp.bfloat16).astype(jnp.float32)
         scaled = d_xnorm * norm_gain
         grad_hidden = (inv_rms * (scaled - x_hat * jnp.mean(scaled * x_hat, axis=-1, keepdims=True)) + dy_f32).astype(jnp.bfloat16)
-        small = [jnp.sum(d_xnorm * x_hat, axis=0), jnp.einsum("te,td->ed", d_logits, xn_f32).reshape(-1)]
+        small = [jnp.sum(d_xnorm * x_hat, axis=0), jnp.einsum("te,td->ed", d_logits, xn_f32).reshape(-1), jnp.pad(jnp.sum(router_probs, axis=0), (0, 128 - n_exp))]
         small = lax.all_gather(jnp.concatenate(small).reshape(-1, 128), all_axes, axis=0, tiled=True)
-        small = jnp.sum(small.reshape(n_dev, -1, 128), axis=0).reshape(1 + n_exp, width)
+        small = jnp.sum(small.reshape(n_dev, -1, 128), axis=0)
+        aux_loss = AUX_COEF * n_exp * jnp.sum(load_frac * small[-1, :n_exp] / total_tok)
+        small = small[:-1].reshape(1 + n_exp, width)
 
         at = n_tile * TILE + SLICE * lax.axis_index("dp")
         wt_mine = lax.dynamic_slice(wt, (0, at, 0), (2, SLICE, width))

time: 605 us -> 626 us (1.035)
  the two profiles are of different devices: /device:TPU:1 before, /device:TPU:6 now
where the time goes in v1:
time: 626 us; the launch traced here: 635 us
  Pallas kernels  428 us (68%)
  waiting for transfers between devices  84.6 us (14%)
  blocking collectives  41 us (7%)
  other arithmetic  30.9 us (5%)
  local copies, waits for them, and re-layouts  25.4 us (4%)
  between operations  17.2 us (3%)
    pallas_call x2, Pallas kernels, tile_grads(): pl.pallas_call(functools.partial(tile_kernel, bool(ff)), grid_spec=pltpu....  283 us
    pallas_call x1, Pallas kernels, own_rows(): pl.pallas_call(own_kernel, grid=(ff // f,), in_specs=[whole, col_spec, co...  66.9 us
    all_to_all x1, waiting for transfers between devices, local_step(): lax.all_to_all(home, 'ep', 0, 0, tiled=True)  52.2 us
    pallas_call x1, Pallas kernels, pack_rows(): pl.pallas_call(pack_kernel, grid_spec=grid_spec, out_shape=[jax.ShapeDtyp...  50.5 us
    all_to_all x1, blocking collectives, local_step(): lax.all_to_all(send, 'ep', 0, 0, tiled=True)  41 us
    all_gather x1, waiting for transfers between devices, local_step(): lax.all_gather(jnp.concatenate([x_norm, grad_out, jnp.pad(expert_ids.asty...  32.3 us
    pallas_call x1, Pallas kernels, place_slices(): pl.pallas_call(place_kernel, grid=(n_part // 2,), in_specs=[pl.BlockSpec(...  27.4 us
  transfers between devices with their start and end apart: 4, of which 2 were waited for; matrix products, arithmetic and copies ran while one was open for 7% of the time, Pallas kernels for 63%

profile of v1, /device:TPU:6, one launch (start us, length us, event | category | flops | bytes accessed | tf_op | source)
XLA Modules:
  0.0 635.2 jit_solution(11250201167654514911)
XLA Ops:
  10.4 1.9 fusion.12
  14.9 2.4 gather_fusion
  18.7 2.4 gather_fusion.1
  21.1 1.5 broadcast_select_fusion
  22.8 41.0 %all_to_all.10 = bf16[8,32,4608]{2,1,0:T(8,128)(2,1)} all-to-all(bf16[8,32,4608]{2,1,0:T(8,128)(2,1)S(1)} %pad_maximum_fusion), channel_id=1, replica_groups=mesh['dp'=16,'ep'=8] {'ep'}, dimensions={0} | all-to-all | bytes 4718592 | tf_op jit(solution)/shard_map/all_to_all | solution.py:338
  63.8 66.9 %own_rows.1 = (bf16[256,4608]{1,0:T(8,128)(2,1)}, bf16[2,5760,2304]{2,1,0:T(8,128)(2,1)}) custom-call(bf16[256,4608]{1,0:T(8,128)(2,1)} %bitcast.61, bf16[2304,5760]{1,0:T(8,128)(2,1)} %bitcast.65, bf16[2304,5760]{1,0:T(8,128)(2,1)} %bitcast.66, bf16[5760,2304]{1,0:T(8,128)(2,1)} %bitcast.63), custom_call_target="tpu_custom_call" | custom-call | flops 40768634880 | bytes 79626240 | tf_op jit(solution)/shard_map/own_rows/pallas_call | solution.py:181
  130.7 6.1 all-to-all-start.1
  137.9 52.2 %all-to-all-done.1 = bf16[8,32,4608]{2,1,0:T(8,128)(2,1)} async-done(((bf16[8,32,4608]{2,1,0:T(8,128)(2,1)}), bf16[8,32,4608]{2,1,0:T(8,128)(2,1)}, u32[]{:S(2)}, u32[]{:S(2)}) %all-to-all-start.1) | async-done | bytes 2359328 | tf_op jit(solution)/shard_map/all_to_all | solution.py:343
  190.2 4.4 gather_fusion.2
  196.1 1.1 fusion.5
  197.3 32.3 %all-gather.6.cloned.1.call-done.tok_hbm = bf16[8192,4736]{1,0:T(8,128)(2,1)} async-done(((bf16[64,4736]{1,0:T(8,128)(2,1)}), bf16[8192,4736]{1,0:T(8,128)(2,1)}) %all-gather.6.cloned.1.call-update) | async-done | bytes 77594640 | tf_op jit(solution)/shard_map/all_gather | solution.py:328
  229.6 2.0 slice_convert_fusion
  231.6 3.3 slice_reduce_fusion.1
  235.3 1.4 fusion.15
  239.6 2.1 dynamic-slice_bitcast_fusion.wd_ref
  241.7 2.8 constant_dynamic-slice_fusion.wt_ref
  244.5 2.5 broadcast_compare_fusion
  247.1 1.8 convert_reduce_fusion
  249.5 2.3 fusion.36
  257.0 50.5 %pack_rows.1 = (bf16[4096,2304]{1,0:T(8,128)(2,1)}, bf16[4096,2304]{1,0:T(8,128)(2,1)}) custom-call(s32[33]{0:T(128)} %get-tuple-element.37.block_of, s32[33]{0:T(128)} %get-tuple-element.36.chunk_of, s32[1]{0:T(128)} %bitcast.18.n_steps, s32[2]{0:T(128)} %pad_add_fusion.1.my_exp, bf16[8192,4736]{1,0:T(8,128)(2,1)} %all-gather.6.cloned.1.call-done.tok_hbm, ...), custom_call_target="tpu_custom_call" | custom-call | flops 24159191040 | bytes 94371840 | tf_op jit(solution)/shard_map/pack_rows/pallas_call | solution.py:114
  307.5 24.4 %slice_grads.1 = bf16[576,2304]{1,0:T(8,128)(2,1)} custom-call(s32[2]{0:T(128)} %pad_add_fusion.n_used, s32[8]{0:T(128)} %get-tuple-element.53.tile_of, s32[8]{0:T(128)} %get-tuple-element.52.block_of, bf16[4096,2304]{1,0:T(8,128)(2,1)} %get-tuple-element.19.x_ref, bf16[4096,2304]{1,0:T(8,128)(2,1)} %get-tuple-element.20.d_ref, ...), custom_call_target="tpu_custom_call" | custom-call | flops 10871635968 | bytes 18874368 | tf_op jit(solution)/shard_map/slice_grads/pallas_call | solution.py:258
  334.3 258.6 %tile_grads.1 = (bf16[2304,5760]{1,0:T(8,128)(2,1)}, bf16[2304,5760]{1,0:T(8,128)(2,1)}, bf16[5760,2304]{1,0:T(8,128)(2,1)}) custom-call(s32[2]{0:T(128)} %pad_add_fusion.2.n_used, s32[56]{0:T(128)} %get-tuple-element.51.tile_of, s32[56]{0:T(128)} %get-tuple-element.50.block_of, bf16[4096,2304]{1,0:T(8,128)(2,1)} %get-tuple-element.19.x_ref, ...), custom_call_target="tpu_custom_call" | custom-call | flops 152202903552 | bytes 132120576 | tf_op jit(solution)/shard_map/tile_grads/pallas_call | solution.py:258
  592.9 4.7 reduce_sum.197
  600.1 27.4 %place_slices.1 = (bf16[2304,5760]{1,0:T(8,128)(2,1)}, bf16[2304,5760]{1,0:T(8,128)(2,1)}, bf16[5760,2304]{1,0:T(8,128)(2,1)}) custom-call(bf16[16,576,2304]{2,1,0:T(8,128)(2,1)} %bitcast.54, bf16[2304,5760]{1,0:T(8,128)(2,1)} %get-tuple-element.22.gg_in, ...), custom_call_target="tpu_custom_call", output_to_operand_aliasing={{0}: (1, {}), {1}: (2, {}), {2}: (3, {})} | custom-call | flops 1000000 | bytes 84934656 | tf_op jit(solution)/shard_map/place_slices/pallas_call | solution.py:292
  (102 shorter events, 21.7 us)
Async XLA Ops:
  7.2 222.4 %all-gather.6.cloned.1.call-start = ((), (), s32[]{:S(2)}) async-start(), calls=%async_computation.2 | async-start | bytes 78200832 | tf_op jit(solution)/shard_map/all_gather | solution.py:328
  9.2 3.0 copy-start.9
  10.4 4.0 copy-start.7
  14.9 2.5 copy-start
  18.7 2.5 copy-start.1
  130.7 59.4 %all-to-all-start.1 = ((bf16[8,32,4608]{2,1,0:T(8,128)(2,1)}), bf16[8,32,4608]{2,1,0:T(8,128)(2,1)}, u32[]{:S(2)}, u32[]{:S(2)}) async-start(bf16[8,32,4608]{2,1,0:T(8,128)(2,1)} %bitcast.60), calls=%async_computation.1 | async-start | bytes 4718592 | tf_op jit(solution)/shard_map/all_to_all | solution.py:343
  136.8 456.1 %all-gather.10.cloned.1.call-start = ((), (), s32[]{:S(2)}) async-start(), calls=%async_computation.4 | async-start | bytes 11096064 | tf_op jit(solution)/shard_map/all_gather | solution.py:359
  195.0 1.1 copy-start.4
  231.6 3.7 copy-start.2
  231.6 3.7 copy-start.8
  235.1 2.6 copy-start.10
  237.6 362.5 %all-gather.8.cloned.1.call-start = ((), (), s32[]{:S(2)}) async-start(), calls=%async_computation.3 | async-start | bytes 45121536 | tf_op jit(solution)/shard_map/all_gather | solution.py:370
  331.9 1.3 copy-start.3
  331.9 1.3 copy-start.5
  331.9 1.3 copy-start.6
  592.9 5.4 copy-start.11
Sparse Core Ops, SparseCore 0:
  12.4 217.1 all-gather.5
  237.7 71.9 all-gather.9
  332.1 243.6 all-gather.7
